TPU v7x, 32 devices: a whole 2x2x4 slice. The times are simulated.
32 devices in a mesh: ep: 8 (over z, y), dp: 4 (over x, core).
Axes of the slice: x: 2, y: 2, z: 4, core: 2. Of those that a mesh axis runs over, the one named last changes fastest.
Arguments:
- tokens: bfloat16 [4096, 7168], P(('dp', 'ep')), parts along dimension 0, may hold values from -18 to 18
- expert_ids: int32 [4096, 2], P(('dp', 'ep')), parts along dimension 0, may hold values from 0 to 3, all different within a row; in each aligned block of 128 rows (0 to 127, 128 to 255, ...) at most 128 rows name the same one
- affinity: float32 [4096, 2], P(('dp', 'ep')), parts along dimension 0, may hold values from 0.05 to 1
- w_gate: bfloat16 [8, 7168, 512], P('ep'), may hold values from -0.0625 to 0.0625
- w_up: bfloat16 [8, 7168, 512], P('ep'), may hold values from -0.0625 to 0.0625
- w_down: bfloat16 [8, 512, 7168], P('ep'), may hold values from -0.1875 to 0.1875
Outputs:
- mixed: bfloat16 [4096, 7168], P(('dp', 'ep')), parts along dimension 0
There are 4 independent parts, one for each index of `dp`. A program takes and returns all parts, laid end to end along the dimension named above; an argument that names none is the same for every part. Nothing has to cross between parts.
Inputs may be any that keep to these rules, and one draw needn't show every extreme that they name: `expert_ids`: each row names 2 different experts; among the rows of one index of ep no expert is named by more than 128 rows.
All inputs are finite; a program needn't handle non-finite values.
Results may differ from a plain program's by a relative error of at most 0.019.
Values may be sent and summed in bfloat16 or wider, within the bound.
A program may use at most 256 MiB of HBM per device.

v0:
```python
import functools

import jax
import jax.numpy as jnp
from jax import lax
from jax.experimental import pallas as pl
from jax.experimental.pallas import tpu as pltpu
from jax.sharding import PartitionSpec as P

LINE = 4
LANES = 128
MESH = pl.DeviceIdType.MESH
VMEM_LIMIT = 48 * 1024 * 1024


def requantized(tokens):
    rows, width = tokens.shape
    blocks = tokens.astype(jnp.float32).reshape(rows, -1, 16)
    largest = jnp.max(jnp.abs(blocks), axis=2)
    scales = (jnp.maximum(largest, 0.25) / 9.0).astype(jnp.bfloat16).astype(jnp.float32)
    divided = blocks / scales[:, :, None]
    payload = jnp.clip(divided, -6.0, 6.0).astype(jnp.bfloat16).astype(jnp.float32)
    return (payload * scales[:, :, None]).astype(jnp.bfloat16).reshape(rows, width)


def split_of(width):
    return width // LANES // 6 * LANES


def halves_of(rows):
    return pl.ds(0, rows // 2), pl.ds(rows // 2, rows // 2)


def meet(targets):
    barrier = pltpu.get_barrier_semaphore()
    for target in targets:
        pl.semaphore_signal(barrier, inc=1, device_id={"ep": target}, device_id_type=MESH)
    pl.semaphore_wait(barrier, len(targets))


def swap(values, lane, distance):
    high = (lane // distance) % 2 == 1
    width = values.shape[1]
    return jnp.where(
        high, pltpu.roll(values, distance, 1), pltpu.roll(values, width - distance, 1)
    )


def quantize_into(tokens_ref, x_ref):
    rows, width = x_ref.shape

    def body(i, carry):
        at = pl.ds(pl.multiple_of(i * LANES, LANES), LANES)
        values = tokens_ref[:, at].astype(jnp.float32)
        lane = lax.broadcasted_iota(jnp.int32, values.shape, 1)
        largest = jnp.abs(values)
        for distance in (1, 2, 4, 8):
            largest = jnp.maximum(largest, swap(largest, lane, distance))
        scales = (jnp.maximum(largest, 0.25) / 9.0).astype(jnp.bfloat16).astype(jnp.float32)
        payload = jnp.clip(values / scales, -6.0, 6.0).astype(jnp.bfloat16).astype(jnp.float32)
        x_ref[:, at] = (payload * scales).astype(x_ref.dtype)
        return carry

    lax.fori_loop(0, width // LANES, body, 0)


class Copies:
    def __init__(self, send, recv):
        self.send, self.recv, self.numbers = send, recv, {}

    def number(self, name):
        return self.numbers.setdefault(name, len(self.numbers))

    def make(self, name, source, place, target):
        k = self.number(name)
        return pltpu.make_async_remote_copy(
            src_ref=source,
            dst_ref=place,
            send_sem=self.send.at[k],
            recv_sem=self.recv.at[k],
            device_id={"ep": target},
            device_id_type=MESH,
        )


def spread(n, tokens_ref, share_ref, all_ref, shares_ref, x_ref, send, recv, local):
    me = lax.axis_index("ep")
    here, y = me // 2, lax.rem(me, 2)
    other = 1 - y
    peer = 2 * here + other
    rows, width = x_ref.shape
    cut = split_of(width)
    first, second = pl.ds(0, cut), pl.ds(cut, width - cut)
    full, halves = pl.ds(0, rows), halves_of(rows)
    quantize_into(tokens_ref, x_ref)
    keep = pltpu.make_async_copy(x_ref, all_ref.at[me], local.at[0])
    keep_share = pltpu.make_async_copy(share_ref, shares_ref.at[me], local.at[1])
    keep.start()
    keep_share.start()
    meet([lax.rem(me + step, n) for step in range(1, n)])
    all_copies = Copies(send, recv)
    shares = [
        all_copies.make(("share", step), share_ref, shares_ref.at[me], lax.rem(me + step, n))
        for step in range(1, n)
    ]
    last = LINE - 1

    def program(z):
        started = []

        def block(owner, side, rows_of, columns):
            return all_ref.at[2 * owner + side, rows_of, columns]

        def start(name, owner, side, rows_of, columns, target, own=False):
            place = block(owner, side, rows_of, columns)
            source = x_ref.at[rows_of, columns] if own else place
            copy = all_copies.make(name, source, place, target)
            copy.start()
            started.append(copy)

        def wait(name, owner, side, rows_of, columns):
            place = block(owner, side, rows_of, columns)
            all_copies.make(name, place, place, peer).wait_recv()

        def onward(kind, owner, side, rows_of, columns, source_z, own=False):
            for way, ok, step in (("up", z < last, 1), ("down", z > 0, -1)):
                if ok and (source_z - z) * step <= 0:
                    start((kind, way, owner), owner, side, rows_of, columns, 2 * (z + step) + y, own)

        def way_of(owner):
            return "up" if owner < z else "down"

        def pass_b(owner, i):
            own = owner == z
            if not own:
                wait((("b", i), way_of(owner), owner), owner, y, halves[i], second)
            onward(("b", i), owner, y, halves[i], second, owner, own)
            start((("b", i), "peer", owner), owner, y, halves[i], second, peer, own)

        def pass_a(kind, owner, side):
            wait((kind, way_of(owner), owner), owner, side, full, first)
            onward(kind, owner, side, full, first, owner)

        start(("a", "peer"), z, y, full, first, peer, True)
        pass_b(z, 0)
        for copy in shares:
            copy.start()
        pass_b(z, 1)
        onward("a", z, y, full, first, z, True)
        by_distance = [
            [owner for owner in (z - hop, z + hop) if 0 <= owner <= last] for hop in range(1, LINE)
        ]
        for hop in range(LINE - 1):
            for i in range(2):
                for owner in by_distance[hop]:
                    pass_b(owner, i)
            if hop == 1:
                wait(("a", "peer"), z, other, full, first)
                onward("p", z, other, full, first, z)
        for owners in by_distance:
            for owner in owners:
                pass_a("a", owner, y)
            for owner in owners:
                pass_a("p", owner, other)
        for owner in range(LINE):
            for i in range(2):
                wait((("b", i), "peer", owner), owner, other, halves[i], second)
        for copy in started:
            copy.wait_send()

    for z in range(LINE):
        pl.when(here == z)(functools.partial(program, z))
    for copy in shares:
        copy.wait()
    keep.wait()
    keep_share.wait()


def all_tokens(tokens, share):
    n = lax.axis_size("ep")
    rows, width = tokens.shape
    count = 64
    return pl.pallas_call(
        functools.partial(spread, n),
        out_shape=(
            jax.ShapeDtypeStruct((n, rows, width), tokens.dtype),
            jax.ShapeDtypeStruct((n,) + share.shape, share.dtype),
        ),
        in_specs=[pl.BlockSpec(memory_space=pltpu.VMEM)] * 2,
        out_specs=[pl.BlockSpec(memory_space=pl.ANY)] * 2,
        scratch_shapes=[
            pltpu.VMEM((rows, width), tokens.dtype),
            pltpu.SemaphoreType.DMA((count,)),
            pltpu.SemaphoreType.DMA((count,)),
            pltpu.SemaphoreType.DMA((2,)),
        ],
        compiler_params=pltpu.CompilerParams(
            collective_id=0, has_side_effects=True, vmem_limit_bytes=VMEM_LIMIT
        ),
        name="spread",
    )(tokens, share)


def add_up(target, sources):
    rows = target.shape[0]
    step = 16

    def body(i, carry):
        at = pl.ds(pl.multiple_of(i * step, step), step)
        total = sources[0][at, :].astype(jnp.float32)
        for source in sources[1:]:
            total = total + source[at, :].astype(jnp.float32)
        target[at, :] = total.astype(target.dtype)
        return carry

    lax.fori_loop(0, rows // step, body, 0)


def gather_sums(
    c_ref, out_ref, own_b, own_a, got_b, zed_b, zed_a, got_a3, send, recv, local
):
    me = lax.axis_index("ep")
    here, y = me // 2, lax.rem(me, 2)
    other = 1 - y
    peer = 2 * here + other
    rows, width = out_ref.shape
    cut = split_of(width)
    first, second = pl.ds(0, cut), pl.ds(cut, width - cut)
    halves = halves_of(rows)
    faces = (other, y)
    last = LINE - 1
    loads = []

    def load(owner, columns, place):
        k = len(loads)
        loads.append(pltpu.make_async_copy(c_ref.at[owner, :, columns], place, local.at[k]))
        loads[k].start()

    for d in range(LINE):
        for i in range(2):
            load(2 * d + faces[i], first, own_a.at[d, i])
    for d in range(LINE):
        load(2 * d + y, second, own_b.at[d])
    meet([lax.rem(me + step, 2 * LINE) for step in range(1, 2 * LINE)])
    all_copies = Copies(send, recv)

    def program(z):
        started = []
        if z in (0, last):
            order = sorted((d for d in range(LINE) if d != z), key=lambda d: -abs(d - z))
        else:
            far, near = (last, 0) if z < last - z else (0, last)
            order = [far, near] + [d for d in range(1, last) if d != z]

        def send_off(name, source, place, target):
            copy = all_copies.make(name, source, place, target)
            copy.start()
            started.append(copy)

        def wait(name, place):
            all_copies.make(name, place, place, peer).wait_recv()

        def feeders(d):
            found = []
            if z > 0 and d >= z:
                found.append(0)
            if z < last and d <= z:
                found.append(1)
            return found

        def take_a(d, i):
            found = feeders(d)
            for way in found:
                wait(("a", way, d, i), zed_a.at[way, d, i])
            return [zed_a.at[way, d, i] for way in found]

        def take_b(d, h):
            wait(("y", d, h), got_b.at[d, halves[h]])
            found = feeders(d)
            for way in found:
                wait(("b", way, d, h), zed_b.at[way, d, halves[h]])
            return [got_b.at[d, halves[h]]] + [zed_b.at[way, d, halves[h]] for way in found]

        def pass_a(d):
            way, target = (0, 2 * (z + 1) + y) if d > z else (1, 2 * (z - 1) + y)
            for i in range(2):
                sources = take_a(d, i)
                if sources:
                    add_up(own_a.at[d, i], [own_a.at[d, i]] + sources)
                send_off(("a", way, d, i), own_a.at[d, i], zed_a.at[way, d, i], target)

        def pass_b(d):
            way, target = (0, 2 * (z + 1) + y) if d > z else (1, 2 * (z - 1) + y)
            for h in range(2):
                mine = own_b.at[d, halves[h]]
                add_up(mine, [mine] + take_b(d, h))
                send_off(("b", way, d, h), mine, zed_b.at[way, d, halves[h]], target)

        for d in order + [z]:
            for h in range(2):
                send_off(
                    ("y", d, h),
                    c_ref.at[2 * d + other, halves[h], second],
                    got_b.at[d, halves[h]],
                    peer,
                )
        for copy in loads:
            copy.wait()
        for d in order:
            pass_a(d)
        rest = order
        if z in (0, last):
            pass_b(order[0])
            rest = order[1:]
        add_up(own_a.at[z, 0], [own_a.at[z, 0]] + take_a(z, 0))
        send_off("a3", own_a.at[z, 0], got_a3, peer)
        ends = take_a(z, 1)
        for d in rest:
            pass_b(d)
        for h in range(2):
            add_up(out_ref.at[halves[h], second], [own_b.at[z, halves[h]]] + take_b(z, h))
        wait("a3", got_a3)
        add_up(out_ref.at[:, first], [own_a.at[z, 1], got_a3] + ends)
        for copy in started:
            copy.wait_send()

    for z in range(LINE):
        pl.when(here == z)(functools.partial(program, z))


def summed(scaled):
    n, rows, width = scaled.shape
    cut = split_of(width)
    rest = width - cut
    kind = scaled.dtype
    count = 48
    return pl.pallas_call(
        gather_sums,
        out_shape=jax.ShapeDtypeStruct((rows, width), kind),
        in_specs=[pl.BlockSpec(memory_space=pl.ANY)],
        out_specs=pl.BlockSpec(memory_space=pltpu.VMEM),
        scratch_shapes=[
            pltpu.VMEM((LINE, rows, rest), kind),
            pltpu.VMEM((LINE, 2, rows, cut), kind),
            pltpu.VMEM((LINE, rows, rest), kind),
            pltpu.VMEM((2, LINE, rows, rest), kind),
            pltpu.VMEM((2, LINE, 2, rows, cut), kind),
            pltpu.VMEM((rows, cut), kind),
            pltpu.SemaphoreType.DMA((count,)),
            pltpu.SemaphoreType.DMA((count,)),
            pltpu.SemaphoreType.DMA((3 * LINE,)),
        ],
        compiler_params=pltpu.CompilerParams(
            collective_id=1, has_side_effects=True, vmem_limit_bytes=VMEM_LIMIT
        ),
        name="gather_sums",
    )(scaled)


def on_device(tokens, expert_ids, affinity, w_gate, w_up, w_down):
    n = lax.axis_size("ep")
    experts = n // 2
    own = lax.axis_index("ep") // 2
    rows, width = tokens.shape
    weights = affinity / jnp.sum(affinity, axis=1, keepdims=True)
    padded = -(-experts // 8) * 8
    names = jnp.arange(padded, dtype=jnp.int32)[:, None]
    shares = sum(
        jnp.where(expert_ids[:, k][None, :] == names, weights[:, k][None, :], 0.0)
        for k in range(weights.shape[1])
    )
    by_line = experts == LINE and rows % 32 == 0 and width % LANES == 0
    if by_line:
        every, shares = all_tokens(tokens, shares)
    else:
        every = lax.all_gather(requantized(tokens), "ep", axis=0, tiled=False)
        shares = lax.all_gather(shares, "ep", axis=0, tiled=False)
    every = every.reshape(n * rows, width)
    share = lax.dynamic_slice_in_dim(shares, own, 1, axis=1).reshape(n * rows, 1)
    gate = jnp.dot(every, w_gate[0], preferred_element_type=jnp.float32)
    upward = jnp.dot(every, w_up[0], preferred_element_type=jnp.float32)
    hidden = (jax.nn.silu(gate) * upward).astype(jnp.bfloat16)
    partial = jnp.dot(hidden, w_down[0], preferred_element_type=jnp.float32)
    scaled = (partial * share).astype(jnp.bfloat16)
    if by_line:
        return summed(scaled.reshape(n, rows, width))
    return lax.psum_scatter(scaled, "ep", scatter_dimension=0, tiled=True)


def solution(mesh):
    in_specs = (
        P(("dp", "ep"), None),
        P(("dp", "ep"), None),
        P(("dp", "ep"), None),
        P("ep", None, None),
        P("ep", None, None),
        P("ep", None, None),
    )
    return jax.shard_map(
        on_device, mesh=mesh, in_specs=in_specs, out_specs=P(("dp", "ep"), None), check_vma=False
    )
```

profile of v0, /device:TPU:16, one launch (start us, length us, event | category | flops | bytes accessed | tf_op | source)
XLA Modules:
  0.0 347.6 jit_solution(353805059606021604)
XLA Ops:
  0.0 0.7 reduce_sum.9
  0.7 0.7 broadcast_divide_fusion
  1.4 0.8 slice_bitcast_fusion.3
  2.2 0.0 copy-start
  2.2 1.5 copy-done
  3.7 163.8 %spread.1 = (bf16[8,128,7168]{2,1,0:T(8,128)(2,1)}, f32[8,8,128]{2,1,0:T(8,128)S(1)}) custom-call(bf16[128,7168]{1,0:T(8,128)(2,1)S(1)} %copy-done, f32[8,128]{1,0:T(8,128)S(1)} %select_add_fusion.share_ref), custom_call_target="tpu_custom_call" | custom-call | tf_op jit(solution)/shard_map/spread/pallas_call | solution.py:183
  167.5 0.0 copy-start.1
  167.5 0.0 copy-start.2
  167.5 13.4 %fusion.1 = f32[1024,512]{1,0:T(8,128)S(1)} fusion(bf16[1024,7168]{1,0:T(8,128)(2,1)} %bitcast.27, bf16[1,7168,512]{2,1,0:T(8,128)(2,1)} %param.10), kind=kOutput, calls=%fused_computation.2 | convolution fusion | flops 7516192768 | bytes 24117248 | tf_op jit(solution)/shard_map/dot_general | solution.py:381
  180.9 0.0 copy-done.1
  180.9 0.3 copy-done.2
  181.2 8.0 %multiply_convert_fusion.1 = bf16[1024,512]{1,0:T(8,128)(2,1)S(1)} fusion(f32[1024,512]{1,0:T(8,128)S(1)} %fusion.1, bf16[1024,7168]{1,0:T(8,128)(2,1)S(1)} %bitcast.28, bf16[1,7168,512]{2,1,0:T(8,128)(2,1)S(1)} %copy-done.2), kind=kOutput, calls=%fused_computation.6 | convolution fusion | flops 7519338496 | bytes 25165824 | tf_op jit(solution)/shard_map/dot_general | solution.py:380
  189.2 14.1 %multiply_convert_fusion = bf16[1024,7168]{1,0:T(8,128)(2,1)} fusion(bf16[1024,512]{1,0:T(8,128)(2,1)S(1)} %multiply_convert_fusion.1, f32[1024]{0:T(1024)S(1)} %bitcast.26, bf16[1,512,7168]{2,1,0:T(8,128)(2,1)} %param.11), kind=kOutput, calls=%fused_computation | convolution fusion | flops 7530872832 | bytes 23072768 | tf_op jit(solution)/shard_map/dot_general | solution.py:383
  203.3 143.1 %gather_sums.1 = bf16[128,7168]{1,0:T(8,128)(2,1)S(1)} custom-call(bf16[8,128,7168]{2,1,0:T(8,128)(2,1)} %bitcast.25), custom_call_target="tpu_custom_call" | custom-call | tf_op jit(solution)/shard_map/gather_sums/pallas_call | solution.py:337
  346.4 1.2 copy.8
  (3 shorter events, 0.0 us)
Async XLA Ops:
  2.2 1.5 copy-start
  167.5 13.4 %copy-start.1 = (bf16[8,128,7168]{2,1,0:T(8,128)(2,1)S(1)}, bf16[8,128,7168]{2,1,0:T(8,128)(2,1)}, u32[]{:S(2)}) copy-start(bf16[8,128,7168]{2,1,0:T(8,128)(2,1)} %get-tuple-element.7) | copy-start | bytes 44040196
  167.5 13.7 %copy-start.2 = (bf16[1,7168,512]{2,1,0:T(8,128)(2,1)S(1)}, bf16[1,7168,512]{2,1,0:T(8,128)(2,1)}, u32[]{:S(2)}) copy-start(bf16[1,7168,512]{2,1,0:T(8,128)(2,1)} %param.9) | copy-start | bytes 22020100
where the time goes:
time: 350 us; the launch traced here: 348 us
  Pallas kernels  307 us (88%)
  matrix products  35.5 us (10%)
  local copies, waits for them, and re-layouts  3.79 us (1%)
    pallas_call x1, Pallas kernels, all_tokens(): pl.pallas_call(functools.partial(spread, n), out_shape=(jax.ShapeDtypeStr...  164 us
    pallas_call x1, Pallas kernels, summed(): pl.pallas_call(gather_sums, out_shape=jax.ShapeDtypeStruct((rows, width),...  143 us
    dot_general x1, matrix products, on_device(): partial = jnp.dot(hidden, w_down[0], preferred_element_type=jnp.float32)  14.1 us
    dot_general x1, matrix products, on_device(): upward = jnp.dot(every, w_up[0], preferred_element_type=jnp.float32)  13.4 us
    dot_general x1, matrix products, on_device(): gate = jnp.dot(every, w_gate[0], preferred_element_type=jnp.float32)  8.02 us

commit v1 on v0

v1 whole, which is shorter than its diff:
```python
import collections
import functools

import jax
import jax.numpy as jnp
from jax import lax
from jax.experimental import pallas as pl
from jax.experimental.pallas import tpu as pltpu
from jax.sharding import PartitionSpec as P

LINE = 4
LANES = 128
MESH = pl.DeviceIdType.MESH
VMEM_LIMIT = 67_000_000
GROUPS = 2
CHUNKS = 4
PARTS = 7
DOWN = 2
PER = CHUNKS // GROUPS
STEPS = LINE * GROUPS
ORDERS = ((3, 2, 1, 0), (3, 0, 2, 1), (0, 3, 1, 2), (0, 1, 2, 3))


def requantized(tokens):
    rows, width = tokens.shape
    blocks = tokens.astype(jnp.float32).reshape(rows, -1, 16)
    largest = jnp.max(jnp.abs(blocks), axis=2)
    scales = (jnp.maximum(largest, 0.25) / 9.0).astype(jnp.bfloat16).astype(jnp.float32)
    divided = blocks / scales[:, :, None]
    payload = jnp.clip(divided, -6.0, 6.0).astype(jnp.bfloat16).astype(jnp.float32)
    return (payload * scales[:, :, None]).astype(jnp.bfloat16).reshape(rows, width)


def swap(values, lane, distance):
    high = (lane // distance) % 2 == 1
    width = values.shape[1]
    return jnp.where(
        high, pltpu.roll(values, distance, 1), pltpu.roll(values, width - distance, 1)
    )


def quantize_at(ref):
    width = ref.shape[1]

    def body(i, carry):
        at = pl.ds(pl.multiple_of(i * LANES, LANES), LANES)
        values = ref[:, at].astype(jnp.float32)
        lane = lax.broadcasted_iota(jnp.int32, values.shape, 1)
        largest = jnp.abs(values)
        for distance in (1, 2, 4, 8):
            largest = jnp.maximum(largest, swap(largest, lane, distance))
        scales = (jnp.maximum(largest, 0.25) / 9.0).astype(jnp.bfloat16).astype(jnp.float32)
        payload = jnp.clip(values / scales, -6.0, 6.0).astype(jnp.bfloat16).astype(jnp.float32)
        ref[:, at] = (payload * scales).astype(ref.dtype)
        return carry

    lax.fori_loop(0, width // LANES, body, 0)


def down_line():
    ready = {z: {(z, c): 0 for c in range(CHUNKS)} for z in range(LINE)}
    sends = {z: [] for z in range(LINE)}
    for slot in range(8 * CHUNKS):
        for z in range(LINE - 1, 0, -1):
            able = [key for key, when in ready[z].items() if when <= slot]
            if able:
                owner, c = min(able, key=lambda key: (-key[0], key[1]))
                del ready[z][owner, c]
                sends[z].append((slot, owner, c))
                if z - 1 > 0:
                    ready[z - 1][owner, c] = slot + 1
    return sends


FIRST, START = -1, 0


def before(k):
    return 1 + 3 * k


def middle(k):
    return 2 + 3 * k


def after(k):
    return 3 + 3 * k


LAST = after(STEPS)


def script(z):
    last = LINE - 1
    down = down_line()
    up = {p: [(slot, last - o, c) for slot, o, c in down[last - p]] for p in range(LINE)}
    moves = [(slot, "down", o, c) for slot, o, c in down[z]]
    moves += [(slot, "up", o, c) for slot, o, c in up[z]]
    arrival = {(z, c): 0 for c in range(CHUNKS)}
    if z < last:
        arrival.update({(o, c): slot + 1 for slot, o, c in down[z + 1]})
    if z > 0:
        arrival.update({(o, c): slot + 1 for slot, o, c in up[z - 1]})
    steps = [(ORDERS[z][k // GROUPS], k % GROUPS) for k in range(STEPS)]
    chunks = [[(o, g * PER + i) for i in range(PER)] for o, g in steps]
    opening = CHUNKS + PER
    raw = []

    def add(place, rank, op):
        raw.append((place, rank, len(raw), op))

    for slot, way, o, c in moves:
        if slot == 0:
            add(FIRST, slot, ("line", way, o, c))
        elif slot <= opening:
            add(START, slot, ("line", way, o, c))
        else:
            add(after((slot - opening - 1) // PER), slot, ("line", way, o, c))
    for i in range(DOWN):
        add(FIRST, 1, ("weights", i))
        add(START, (i + 1) * CHUNKS / DOWN + 0.6, ("weights y", i))
    add(START, CHUNKS / DOWN * 2 + 1.1, ("weights x", 0))
    for i in range(1, DOWN):
        add(START if i < DOWN - 1 else before(0), 99, ("weights x", i))
    latest = 0
    for o, c in chunks[0] + chunks[1][:1]:
        latest = max(latest, arrival[o, c] + 0.2)
        add(START, latest, ("cross", o, c))
    for k in range(STEPS):
        o, g = steps[k]
        for o, c in chunks[k]:
            add(before(k), 0, ("arrived", o, c))
            add(before(k), 1, ("crossed", o, c))
            add(middle(k), 2, ("free", o, c))
        if k + 1 < STEPS:
            for o, c in chunks[k + 1][1:]:
                add(middle(k), 0, ("cross", o, c))
        if k + 2 < STEPS:
            add(after(k), -1, ("cross",) + chunks[k + 2][0])
    if 0 < z < last:
        far, back, near = ORDERS[z][:3]
        for k, o, g in (
            (1, far, 0),
            (2, far, 1),
            (3, back, 0),
            (4, back, 1),
            (4, near, 0),
            (5, near, 1),
        ):
            add(after(k), 99, ("add", o, g))
    for g in range(GROUPS):
        add(after(STEPS - GROUPS + g), 100, ("finish", g))
    waited, sent, freed = set(), set(), set()
    done = collections.defaultdict(list)
    for place, rank, number, op in sorted(raw):
        out = done[place]
        if op[0] in ("line", "cross", "arrived"):
            key = op[-2:]
            if key[0] != z and key not in waited:
                waited.add(key)
                out.append(("wait",) + key)
        if op[0] == "arrived":
            continue
        if op[0] in ("line", "cross"):
            assert op[-2:] not in freed
            sent.add((op[1] if op[0] == "line" else "cross",) + op[-2:])
        if op[0] == "free":
            freed.add(op[-2:])
            for way in ("up", "down", "cross"):
                if (way,) + op[-2:] in sent:
                    out.append(("sent", way) + op[-2:])
            continue
        out.append(op)
    assert len(freed) == LINE * CHUNKS
    return done


def layer(
    tokens_ref,
    share_ref,
    gate_ref,
    up_ref,
    down_ref,
    out_ref,
    x_ref,
    wg_ref,
    wu_ref,
    wd_ref,
    hid_ref,
    peer_ref,
    got_ref,
    shares_ref,
    local,
    line_send,
    line_recv,
    cross_send,
    cross_recv,
    hid_send,
    hid_recv,
    part_send,
    part_recv,
    share_send,
    share_recv,
    w_send,
    w_recv,
):
    me, dp = lax.axis_index("ep"), lax.axis_index("dp")
    here, y = me // 2, lax.rem(me, 2)
    other = 1 - y
    last = LINE - 1
    peer = {"ep": 2 * here + other}
    twin = {"dp": dp + 1 - 2 * lax.rem(dp, 2)}
    across = {"dp": lax.rem(dp + 2, 4)}
    rows, width = out_ref.shape
    lot = rows // GROUPS
    size = rows // CHUNKS
    part = width // PARTS
    inner = wg_ref.shape[1]
    scripts = [script(z) for z in range(LINE)]

    def chunk(o, c):
        g, i = c // PER, c % PER
        return x_ref.at[o, g, pl.ds(pl.multiple_of(y * lot + i * size, size), size), :]

    def crossing(o, c):
        g, i = c // PER, c % PER
        return x_ref.at[o, g, pl.ds(pl.multiple_of(other * lot + i * size, size), size), :]

    def remote(source, place, send, recv, target):
        return pltpu.make_async_remote_copy(
            src_ref=source,
            dst_ref=place,
            send_sem=send,
            recv_sem=recv,
            device_id=target,
            device_id_type=MESH,
        )

    def line(way, o, c):
        target = {"ep": me + 2 if way == "up" else me - 2}
        place = chunk(o, c)
        return remote(
            place, place, line_send.at[0 if way == "up" else 1, o, c], line_recv.at[o, c], target
        )

    def cross(o, c):
        place = chunk(o, c)
        return remote(place, place, cross_send.at[o, c], cross_recv.at[o, c], peer)

    quarter = down_ref.shape[1] // 4
    piece = quarter // DOWN

    def rows_of(q, i):
        return pl.ds(pl.multiple_of(q * quarter + i * piece, piece), piece)

    def weight(kind, half, q, i, target):
        place = wd_ref.at[half, rows_of(q, i), :]
        source = down_ref.at[0, rows_of(q, i), :] if kind == 0 else place
        return remote(source, place, w_send.at[kind, i], w_recv.at[kind, i], target)

    q_mine, q_across = dp, lax.rem(dp + 2, 4)
    twin_dp = dp + 1 - 2 * lax.rem(dp, 2)
    q_twin, q_twin_across = twin_dp, lax.rem(twin_dp + 2, 4)

    def partial(z, o, g, n, way):
        step = 1 if way == "up" else -1
        nearest = isinstance(z, int) and z + step == o
        slot = LINE if way == "down" and nearest else o
        return part_copy(o, slot, g, n, {"ep": me + 2 * step})

    def part_copy(o, slot, g, n, target):
        columns = pl.ds(pl.multiple_of(n * part, part), part)
        source = x_ref.at[o, g, pl.ds(pl.multiple_of(y * lot, lot), lot), columns]
        return remote(
            source,
            got_ref.at[slot, g, :, columns],
            part_send.at[o, g, n],
            part_recv.at[slot, g, n],
            target,
        )

    def got_wait(slot, g, n):
        columns = pl.ds(pl.multiple_of(n * part, part), part)
        place = got_ref.at[slot, g, :, columns]
        remote(place, place, part_send.at[0, g, n], part_recv.at[slot, g, n], peer).wait_recv()

    def sum_into(target, at, sources):
        step = 16

        def body(i, carry):
            lines = pl.ds(pl.multiple_of(i * step, step), step)
            total = sources[0][lines, at].astype(jnp.float32)
            for source in sources[1:]:
                total = total + source[lines, at].astype(jnp.float32)
            target[lines, at] = total.astype(target.dtype)
            return carry

        lax.fori_loop(0, lot // step, body, 0)

    def run(z, op):
        kind = op[0]
        if kind == "wait":
            line("up", *op[1:]).wait_recv()
        elif kind == "line":
            line(*op[1:]).start()
        elif kind == "cross":
            cross(*op[1:]).start()
        elif kind == "crossed":
            place = crossing(*op[1:])
            o, c = op[1:]
            remote(place, place, cross_send.at[o, c], cross_recv.at[o, c], peer).wait_recv()
        elif kind == "sent":
            way, o, c = op[1:]
            (cross(o, c) if way == "cross" else line(way, o, c)).wait_send()
        elif kind == "weights":
            weight(0, y, q_mine, op[1], peer).start()
        elif kind == "weights y":
            weight(0, other, q_mine, op[1], peer).wait_recv()
            weight(1, other, q_mine, op[1], across).start()
            weight(2, other, q_mine, op[1], twin).start()
        elif kind == "weights x":
            weight(1, other, q_across, op[1], across).wait_recv()
            weight(3, other, q_across, op[1], twin).start()
        elif kind == "add":
            o, g = op[1:]
            mine = x_ref.at[o, g, pl.ds(pl.multiple_of(y * lot, lot), lot), :]

            def body(n, carry):
                got_wait(o, g, n)
                at = pl.ds(pl.multiple_of(n * part, part), part)
                sum_into(mine, at, [mine, got_ref.at[o, g]])
                partial(z, o, g, n, "up" if o > z else "down").start()
                return carry

            lax.fori_loop(0, PARTS, body, 0)
        elif kind == "finish":
            g = op[1]
            mine = x_ref.at[z, g, pl.ds(pl.multiple_of(y * lot, lot), lot), :]
            slots = ([z] if z > 0 else []) + ([LINE] if z < last else [])

            def body(n, carry):
                for slot in slots:
                    got_wait(slot, g, n)
                at = pl.ds(pl.multiple_of(n * part, part), part)
                sum_into(
                    out_ref.at[pl.ds(g * lot, lot), :],
                    at,
                    [mine] + [got_ref.at[slot, g] for slot in slots],
                )
                return carry

            lax.fori_loop(0, PARTS, body, 0)
        else:
            raise ValueError(kind)

    def play(place):
        for z in range(LINE):
            ops = scripts[z][place]
            if ops:

                @pl.when(here == z)
                def _(z=z, ops=ops):
                    for op in ops:
                        run(z, op)

    def play_in(kind, k):
        for z in range(LINE):

            @pl.when(here == z)
            def _(z=z):
                for step in range(STEPS):
                    ops = scripts[z][kind(step)]
                    if ops:

                        @pl.when(k == step)
                        def _(ops=ops):
                            for op in ops:
                                run(z, op)

    own_rows = pl.ds(pl.multiple_of(y * lot, lot), lot)
    loads = []

    def load(source, place):
        copy = pltpu.make_async_copy(source, place, local.at[len(loads)])
        loads.append(copy)
        copy.start()

    for g in range(GROUPS):
        load(tokens_ref.at[pl.ds(g * lot, lot), :], x_ref.at[here, g, own_rows, :])
    load(gate_ref.at[0], wg_ref)
    load(up_ref.at[0], wu_ref)
    load(down_ref.at[0], wd_ref.at[y])
    barrier = pltpu.get_barrier_semaphore()
    targets = [{"ep": lax.rem(me + 2 * step, 2 * LINE)} for step in range(1, LINE)]
    targets += [peer, twin, across]
    for target in targets:
        pl.semaphore_signal(barrier, inc=1, device_id=target, device_id_type=MESH)

    def quantize(c):
        g, i = c // PER, c % PER
        if i == 0:
            loads[g].wait()
        quantize_at(chunk(here, c))

    quantize(0)
    pl.semaphore_wait(barrier, len(targets))
    play(FIRST)
    shares = []
    for step in range(1, LINE):
        target = {"ep": lax.rem(me + 2 * step, 2 * LINE)}
        copy = remote(
            share_ref, shares_ref.at[here], share_send.at[step], share_recv.at[step], target
        )
        copy.start()
        shares.append(copy)
    shares_ref[here] = share_ref[...]
    for c in range(1, CHUNKS):
        quantize(c)
    play(START)
    for copy in loads[GROUPS:]:
        copy.wait()
    for copy in shares:
        copy.wait()

    def order(k):
        b = k // GROUPS
        value = jnp.int32(0)
        for z in range(LINE):
            for i in range(LINE):
                value = jnp.where((here == z) & (b == i), ORDERS[z][i], value)
        return value

    half = inner // 2

    def step_of(k, carry):
        o, g = order(k), lax.rem(k, GROUPS)
        play_in(before, k)

        def hidden(j, c):
            at = pl.ds(pl.multiple_of(j * half, half), half)
            x = x_ref[o, g]
            gate = jnp.dot(x, wg_ref[:, at], preferred_element_type=jnp.float32)
            upward = jnp.dot(x, wu_ref[:, at], preferred_element_type=jnp.float32)
            hid_ref[o, g, :, at] = (jax.nn.silu(gate) * upward).astype(hid_ref.dtype)
            return c

        lax.fori_loop(0, 2, hidden, 0)
        other_rows = pl.ds(pl.multiple_of(other * lot, lot), lot)
        back = remote(
            hid_ref.at[o, g, other_rows, :],
            peer_ref.at[o, g],
            hid_send.at[o, g],
            hid_recv.at[o, g],
            peer,
        )
        back.start()
        play_in(middle, k)

        @pl.when(k == 0)
        def _():
            for i in range(DOWN):
                weight(2, other, q_twin, i, twin).wait_recv()
                weight(3, other, q_twin_across, i, twin).wait_recv()

        back.wait()
        row = shares_ref[o, pl.ds(here, 1), :]
        square = (lot, row.shape[1])
        lane = lax.broadcasted_iota(jnp.int32, square, 1)
        line_of = lax.broadcasted_iota(jnp.int32, square, 0)
        share = jnp.sum(
            jnp.where(lane == line_of + g * lot, jnp.broadcast_to(row, square), 0.0),
            axis=1,
            keepdims=True,
        )
        begins = ((here == 0) & (o != 0)) | ((here == last) & (o != last))
        slot = jnp.where((here == last) & (o == last - 1), LINE, o)
        onward = jnp.where(here == 0, me + 2, me - 2)

        def down(n, c):
            at = pl.ds(pl.multiple_of(n * part, part), part)
            total = jnp.dot(
                hid_ref[o, g, own_rows, :], wd_ref[y, :, at], preferred_element_type=jnp.float32
            ) + jnp.dot(peer_ref[o, g], wd_ref[other, :, at], preferred_element_type=jnp.float32)
            x_ref[o, g, own_rows, at] = (total * share).astype(x_ref.dtype)

            @pl.when(begins)
            def _():
                part_copy(o, slot, g, n, {"ep": onward}).start()

            return c

        lax.fori_loop(0, PARTS, down, 0)
        play_in(after, k)
        return carry

    lax.fori_loop(0, STEPS, step_of, 0)

    def drain(i, carry):
        o, g = i // GROUPS, lax.rem(i, GROUPS)

        @pl.when(o != here)
        def _():
            def body(n, c):
                part_copy(o, o, g, n, peer).wait_send()
                return c

            lax.fori_loop(0, PARTS, body, 0)

        return carry

    lax.fori_loop(0, STEPS, drain, 0)
    for i in range(DOWN):
        weight(0, y, q_mine, i, peer).wait_send()
        weight(1, other, q_mine, i, across).wait_send()
        weight(2, other, q_mine, i, twin).wait_send()
        weight(3, other, q_across, i, twin).wait_send()


def fused(tokens, share, w_gate, w_up, w_down):
    rows, width = tokens.shape
    inner = w_gate.shape[2]
    lot = rows // GROUPS
    kind = tokens.dtype
    dma = pltpu.SemaphoreType.DMA
    anywhere = pl.BlockSpec(memory_space=pl.ANY)
    inside = pl.BlockSpec(memory_space=pltpu.VMEM)
    return pl.pallas_call(
        layer,
        out_shape=jax.ShapeDtypeStruct((rows, width), kind),
        in_specs=[anywhere, inside, anywhere, anywhere, anywhere],
        out_specs=inside,
        scratch_shapes=[
            pltpu.VMEM((LINE, GROUPS, 2 * lot, width), kind),
            pltpu.VMEM((width, inner), kind),
            pltpu.VMEM((width, inner), kind),
            pltpu.VMEM((2, inner, width), kind),
            pltpu.VMEM((LINE, GROUPS, 2 * lot, inner), kind),
            pltpu.VMEM((LINE, GROUPS, lot, inner), kind),
            pltpu.VMEM((LINE + 1, GROUPS, lot, width), kind),
            pltpu.VMEM((LINE,) + share.shape, share.dtype),
            dma((GROUPS + 3,)),
            dma((2, LINE, CHUNKS)),
            dma((LINE, CHUNKS)),
            dma((LINE, CHUNKS)),
            dma((LINE, CHUNKS)),
            dma((LINE, GROUPS)),
            dma((LINE, GROUPS)),
            dma((LINE, GROUPS, PARTS)),
            dma((LINE + 1, GROUPS, PARTS)),
            dma((LINE,)),
            dma((LINE,)),
            dma((4, DOWN)),
            dma((4, DOWN)),
        ],
        compiler_params=pltpu.CompilerParams(
            collective_id=0, has_side_effects=True, vmem_limit_bytes=VMEM_LIMIT
        ),
        name="layer",
    )(tokens, share, w_gate, w_up, w_down)


def on_device(tokens, expert_ids, affinity, w_gate, w_up, w_down):
    n = lax.axis_size("ep")
    experts = n // 2
    own = lax.axis_index("ep") // 2
    rows, width = tokens.shape
    weights = affinity / jnp.sum(affinity, axis=1, keepdims=True)
    padded = -(-experts // 8) * 8
    names = jnp.arange(padded, dtype=jnp.int32)[:, None]
    shares = sum(
        jnp.where(expert_ids[:, k][None, :] == names, weights[:, k][None, :], 0.0)
        for k in range(weights.shape[1])
    )
    by_line = (
        experts == LINE
        and lax.axis_size("dp") == 4
        and rows == LANES
        and width % (PARTS * LANES) == 0
    )
    if by_line:
        return fused(tokens, shares, w_gate, w_up, w_down)
    every = lax.all_gather(requantized(tokens), "ep", axis=0, tiled=False)
    shares = lax.all_gather(shares, "ep", axis=0, tiled=False)
    every = every.reshape(n * rows, width)
    share = lax.dynamic_slice_in_dim(shares, own, 1, axis=1).reshape(n * rows, 1)
    gate = jnp.dot(every, w_gate[0], preferred_element_type=jnp.float32)
    upward = jnp.dot(every, w_up[0], preferred_element_type=jnp.float32)
    hidden = (jax.nn.silu(gate) * upward).astype(jnp.bfloat16)
    partial = jnp.dot(hidden, w_down[0], preferred_element_type=jnp.float32)
    scaled = (partial * share).astype(jnp.bfloat16)
    return lax.psum_scatter(scaled, "ep", scatter_dimension=0, tiled=True)


def solution(mesh):
    in_specs = (
        P(("dp", "ep"), None),
        P(("dp", "ep"), None),
        P(("dp", "ep"), None),
        P("ep", None, None),
        P("ep", None, None),
        P("ep", None, None),
    )
    return jax.shard_map(
        on_device, mesh=mesh, in_specs=in_specs, out_specs=P(("dp", "ep"), None), check_vma=False
    )
```

time: 350 us -> 286 us (0.82)
  matrix products: 35.5 us -> 0 us
  Pallas kernels: 307 us -> 279 us
    dot_general x3 -> x0, matrix products: 35.5 us -> none  [the longest x1 14.1 us: on_device(): partial = jnp.dot(hidden, w_down[0], preferred_element_type=jnp.float32)]
    pallas_call x2 -> x1, Pallas kernels: 307 us -> 279 us  [fused(): pl.pallas_call(layer, out_shape=jax.ShapeDtypeStruct((rows, width), kind)...]
where the time goes in v1:
time: 286 us; the launch traced here: 284 us
  Pallas kernels  279 us (98%)
  local copies, waits for them, and re-layouts  3.61 us (1%)
    pallas_call x1, Pallas kernels, fused(): pl.pallas_call(layer, out_shape=jax.ShapeDtypeStruct((rows, width), kind)...  279 us

profile of v1, /device:TPU:16, one launch (start us, length us, event | category | flops | bytes accessed | tf_op | source)
XLA Modules:
  0.0 284.3 jit_solution(7045584363519356973)
XLA Ops:
  0.0 0.7 reduce_sum.9
  0.7 0.7 broadcast_divide_fusion
  1.4 0.8 slice_bitcast_fusion.3
  2.1 0.6 select_add_fusion.share_ref
  2.7 278.7 %layer.1 = bf16[128,7168]{1,0:T(8,128)(2,1)} custom-call(bf16[128,7168]{1,0:T(8,128)(2,1)} %tokens_ref.1, f32[8,128]{1,0:T(8,128)} %select_add_fusion.share_ref, bf16[1,7168,512]{2,1,0:T(8,128)(2,1)} %gate_ref.1, bf16[1,7168,512]{2,1,0:T(8,128)(2,1)} %up_ref.1, bf16[1,512,7168]{2,1,0:T(8,128)(2,1)} %down_ref.1), custom_call_target="tpu_custom_call" | custom-call | tf_op jit(solution)/shard_map/layer/pallas_call | solution.py:527
  281.5 2.8 %copy.8 = bf16[128,7168]{1,0:T(8,128)(2,1)} copy(bf16[128,7168]{1,0:T(8,128)(2,1)} %layer.1) | data formatting | bytes 3670016
  (1 shorter events, 0.0 us)

commit v2 on v1

--- a/solution.py
+++ b/solution.py
@@ -11,13 +11,19 @@
 LINE = 4
 LANES = 128
 MESH = pl.DeviceIdType.MESH
-VMEM_LIMIT = 67_000_000
+VMEM_LIMIT = 62_000_000
 GROUPS = 2
-CHUNKS = 4
+CHUNKS = 8
+EARLY = ()
 PARTS = 7
+BLOCKS = 4
+LEAD = 0.5
+SLACK = 0.3
 DOWN = 2
 PER = CHUNKS // GROUPS
 STEPS = LINE * GROUPS
+PIECES = CHUNKS + len(EARLY)
+AHEAD = sorted({c * BLOCKS // CHUNKS for c in (0, *EARLY)})
 ORDERS = ((3, 2, 1, 0), (3, 0, 2, 1), (0, 3, 1, 2), (0, 1, 2, 3))
 
 
@@ -31,48 +37,75 @@
     return (payload * scales[:, :, None]).astype(jnp.bfloat16).reshape(rows, width)
 
 
-def swap(values, lane, distance):
-    high = (lane // distance) % 2 == 1
-    width = values.shape[1]
-    return jnp.where(
-        high, pltpu.roll(values, distance, 1), pltpu.roll(values, width - distance, 1)
-    )
-
-
 def quantize_at(ref):
-    width = ref.shape[1]
+    rows, width = ref.shape
+    many = PARTS
+    square = (LANES, LANES)
+    source = lax.broadcasted_iota(jnp.int32, square, 0)
+    target = lax.broadcasted_iota(jnp.int32, square, 1)
+    spread = jnp.where(source == target // 16 * 16 + 15, 1.0, 0.0).astype(ref.dtype)
 
     def body(i, carry):
-        at = pl.ds(pl.multiple_of(i * LANES, LANES), LANES)
-        values = ref[:, at].astype(jnp.float32)
-        lane = lax.broadcasted_iota(jnp.int32, values.shape, 1)
-        largest = jnp.abs(values)
-        for distance in (1, 2, 4, 8):
-            largest = jnp.maximum(largest, swap(largest, lane, distance))
-        scales = (jnp.maximum(largest, 0.25) / 9.0).astype(jnp.bfloat16).astype(jnp.float32)
-        payload = jnp.clip(values / scales, -6.0, 6.0).astype(jnp.bfloat16).astype(jnp.float32)
-        ref[:, at] = (payload * scales).astype(ref.dtype)
+        tiles, tops = [], []
+        for u in range(many):
+            at = pl.ds(pl.multiple_of((i * many + u) * LANES, LANES), LANES)
+            values = ref[:, at]
+            tiles.append((at, values))
+            top = jnp.abs(values)
+            for distance in (1, 2, 4, 8):
+                top = jnp.maximum(top, pltpu.roll(top, distance, 1))
+            tops.append(top)
+        largest = jnp.dot(
+            jnp.concatenate(tops, axis=0), spread, preferred_element_type=jnp.float32
+        )
+        results = []
+        for u in range(many):
+            at, values = tiles[u]
+            scales = jnp.maximum(largest[u * rows : (u + 1) * rows], 0.25) / 9.0
+            scales = scales.astype(jnp.bfloat16).astype(jnp.float32)
+            payload = jnp.clip(values.astype(jnp.float32) / scales, -6.0, 6.0)
+            payload = payload.astype(jnp.bfloat16).astype(jnp.float32)
+            results.append((payload * scales).astype(ref.dtype))
+        for u in range(many):
+            ref[:, tiles[u][0]] = results[u]
         return carry
 
-    lax.fori_loop(0, width // LANES, body, 0)
+    lax.fori_loop(0, width // LANES // many, body, 0)
+
+
+def row_of(piece):
+    return piece if piece < CHUNKS else EARLY[piece - CHUNKS]
+
+
+def in_order():
+    return sorted(range(PIECES), key=lambda piece: (row_of(piece) // PER, piece))
 
 
 def down_line():
-    ready = {z: {(z, c): 0 for c in range(CHUNKS)} for z in range(LINE)}
+    ranks = {piece: rank for rank, piece in enumerate(in_order())}
+    ready = {
+        z: {(z, piece): max(0, piece - CHUNKS + 2) for piece in range(PIECES)}
+        for z in range(LINE)
+    }
     sends = {z: [] for z in range(LINE)}
-    for slot in range(8 * CHUNKS):
+    for slot in range(8 * PIECES):
         for z in range(LINE - 1, 0, -1):
             able = [key for key, when in ready[z].items() if when <= slot]
             if able:
-                owner, c = min(able, key=lambda key: (-key[0], key[1]))
-                del ready[z][owner, c]
-                sends[z].append((slot, owner, c))
+                owner, piece = min(able, key=lambda key: (-key[0], ranks[key[1]]))
+                del ready[z][owner, piece]
+                sends[z].append((slot, owner, piece))
                 if z - 1 > 0:
-                    ready[z - 1][owner, c] = slot + 1
+                    ready[z - 1][owner, piece] = slot + 1
     return sends
 
 
+def flip(order):
+    return tuple(LINE - 1 - owner for owner in order)
+
+
 FIRST, START = -1, 0
+BACK = 4 * 512 / 7168 / GROUPS * CHUNKS / LINE
 
 
 def before(k):
@@ -88,6 +121,51 @@
 
 
 LAST = after(STEPS)
+
+
+def crossings(g):
+    return [c for c in range(g * PER, g * PER + PER) if c not in EARLY]
+
+
+def due(k):
+    each = [len(crossings(g)) + BACK for g in range(GROUPS)]
+    return LEAD + len(EARLY) + CHUNKS + k // GROUPS * sum(each) + sum(each[: k % GROUPS + 1])
+
+
+def ready_at(k):
+    return due(k) + 2
+
+
+def gap_of(time, least):
+    k = least
+    while k < STEPS - 1 and due(k + 1) - SLACK < time:
+        k += 1
+    return k
+
+
+def climb(orders):
+    down = down_line()
+    took = CHUNKS / GROUPS / PARTS
+    came = {z: {} for z in range(LINE)}
+    adds = {z: [] for z in range(LINE)}
+    for z in range(LINE - 1):
+        free = max(slot for slot, o, piece in down[LINE - 1 - z]) + 1
+        todo = []
+        for k in range(STEPS):
+            o, g = orders[z][k // GROUPS], k % GROUPS
+            if o > z:
+                for n in range(PARTS):
+                    when = ready_at(k) + 0.1 * n
+                    place = k
+                    if z > 0:
+                        place = gap_of(came[z][o, g, n], k)
+                        when = max(came[z][o, g, n], ready_at(place))
+                    todo.append((place, when, o, g, n))
+        for place, when, o, g, n in sorted(todo):
+            free = max(free, when) + took
+            came[z + 1][o, g, n] = free + 0.3
+            adds[z].append((place, when, o, g, n))
+    return came, adds
 
 
 def script(z):
@@ -102,82 +180,117 @@
     if z > 0:
         arrival.update({(o, c): slot + 1 for slot, o, c in up[z - 1]})
     steps = [(ORDERS[z][k // GROUPS], k % GROUPS) for k in range(STEPS)]
-    chunks = [[(o, g * PER + i) for i in range(PER)] for o, g in steps]
-    opening = CHUNKS + PER
+    chunks = [[(o, c) for c in crossings(g)] for o, g in steps]
     raw = []
 
     def add(place, rank, op):
         raw.append((place, rank, len(raw), op))
 
-    for slot, way, o, c in moves:
+    for i, c in enumerate(EARLY):
+        add(FIRST, 0.5, ("cross", z, c))
+    for slot, way, o, piece in moves:
         if slot == 0:
-            add(FIRST, slot, ("line", way, o, c))
-        elif slot <= opening:
-            add(START, slot, ("line", way, o, c))
+            add(FIRST, 0, ("line", way, o, piece))
+        elif slot <= due(0) - SLACK:
+            add(START, slot, ("line", way, o, piece))
         else:
-            add(after((slot - opening - 1) // PER), slot, ("line", way, o, c))
+            add(after(min(STEPS - 2, gap_of(slot, 0))), slot, ("line", way, o, piece))
+    for i in range(BLOCKS):
+        if i not in AHEAD:
+            add(START, i * CHUNKS / BLOCKS - 0.8, ("quantize", i))
+    slow = CHUNKS / DOWN
     for i in range(DOWN):
         add(FIRST, 1, ("weights", i))
-        add(START, (i + 1) * CHUNKS / DOWN + 0.6, ("weights y", i))
-    add(START, CHUNKS / DOWN * 2 + 1.1, ("weights x", 0))
-    for i in range(1, DOWN):
-        add(START if i < DOWN - 1 else before(0), 99, ("weights x", i))
+        add(START, len(EARLY) + (i + 1) * slow + 0.6, ("weights y", i))
+        when = len(EARLY) + (i + 2) * slow + 1.1
+        add(START if when < due(0) else before(0), when, ("weights x", i))
     latest = 0
     for o, c in chunks[0] + chunks[1][:1]:
         latest = max(latest, arrival[o, c] + 0.2)
         add(START, latest, ("cross", o, c))
     for k in range(STEPS):
         o, g = steps[k]
-        for o, c in chunks[k]:
+        for c in range(g * PER, g * PER + PER):
             add(before(k), 0, ("arrived", o, c))
-            add(before(k), 1, ("crossed", o, c))
+            if c in EARLY and o != z:
+                add(before(k), 0.5, ("arrived", o, CHUNKS + EARLY.index(c)))
+            else:
+                add(before(k), 1, ("crossed", o, c))
             add(middle(k), 2, ("free", o, c))
         if k + 1 < STEPS:
             for o, c in chunks[k + 1][1:]:
                 add(middle(k), 0, ("cross", o, c))
         if k + 2 < STEPS:
             add(after(k), -1, ("cross",) + chunks[k + 2][0])
-    if 0 < z < last:
-        far, back, near = ORDERS[z][:3]
-        for k, o, g in (
-            (1, far, 0),
-            (2, far, 1),
-            (3, back, 0),
-            (4, back, 1),
-            (4, near, 0),
-            (5, near, 1),
-        ):
-            add(after(k), 99, ("add", o, g))
+    flipped = [flip(ORDERS[last - p]) for p in range(LINE)]
+    came_up, adds_up = climb(ORDERS)
+    came_down, adds_down = climb(flipped)
+    came, adds = {}, []
+    if z > 0:
+        for key, when in came_up[z].items():
+            came[key] = max(came.get(key, 0), when)
+        if z < last:
+            adds += adds_up[z]
+    if z < last:
+        for (o, g, n), when in came_down[last - z].items():
+            came[last - o, g, n] = max(came.get((last - o, g, n), 0), when)
+        if z > 0:
+            adds += [(k, when, last - o, g, n) for k, when, o, g, n in adds_down[last - z]]
+    for k, when, o, g, n in sorted(adds):
+        add(after(k), when, ("add", o, g, n))
     for g in range(GROUPS):
-        add(after(STEPS - GROUPS + g), 100, ("finish", g))
-    waited, sent, freed = set(), set(), set()
+        own = [k for k in range(STEPS) if steps[k] == (z, g)][0]
+        for n in range(PARTS):
+            k = gap_of(came[z, g, n], own)
+            add(after(k), max(came[z, g, n], ready_at(k)), ("finish", z, g, n))
+    waited, sent, freed = set(), [], set()
     done = collections.defaultdict(list)
     for place, rank, number, op in sorted(raw):
         out = done[place]
-        if op[0] in ("line", "cross", "arrived"):
-            key = op[-2:]
-            if key[0] != z and key not in waited:
+        kind, key = op[0], op[-2:]
+        if kind in ("add", "finish"):
+            if out and out[-1][:3] == op[:3] and out[-1][4] == op[3]:
+                out[-1] = out[-1][:4] + (op[3] + 1,)
+            else:
+                out.append(op + (op[3] + 1,))
+            continue
+        if kind in ("line", "cross", "arrived") and key not in waited:
+            if key[0] != z:
                 waited.add(key)
                 out.append(("wait",) + key)
-        if op[0] == "arrived":
+            elif key[1] >= CHUNKS:
+                waited.add(key)
+                out.append(("crossed", z, EARLY[key[1] - CHUNKS]))
+        if kind == "crossed":
+            early = EARLY.index(key[1]) + CHUNKS if key[1] in EARLY else None
+            if early is not None and key[0] == z:
+                if (z, early) not in waited:
+                    waited.add((z, early))
+                    out.append(op)
+                continue
+        if kind == "arrived":
             continue
-        if op[0] in ("line", "cross"):
-            assert op[-2:] not in freed
-            sent.add((op[1] if op[0] == "line" else "cross",) + op[-2:])
-        if op[0] == "free":
-            freed.add(op[-2:])
-            for way in ("up", "down", "cross"):
-                if (way,) + op[-2:] in sent:
-                    out.append(("sent", way) + op[-2:])
+        if kind in ("line", "cross"):
+            assert key not in freed
+            sent.append((op[1] if kind == "line" else "cross",) + key)
+        if kind == "free":
+            freed.add(key)
+            for item in list(sent):
+                if item[1:] == key:
+                    sent.remove(item)
+                    out.append(("sent",) + item)
             continue
         out.append(op)
     assert len(freed) == LINE * CHUNKS
+    for item in sent:
+        done[LAST].append(("sent",) + item)
     return done
 
 
 def layer(
     tokens_ref,
-    share_ref,
+    ids_ref,
+    affinity_ref,
     gate_ref,
     up_ref,
     down_ref,
@@ -238,7 +351,7 @@
 
     def line(way, o, c):
         target = {"ep": me + 2 if way == "up" else me - 2}
-        place = chunk(o, c)
+        place = chunk(o, c) if c < CHUNKS else crossing(o, EARLY[c - CHUNKS])
         return remote(
             place, place, line_send.at[0 if way == "up" else 1, o, c], line_recv.at[o, c], target
         )
@@ -296,6 +409,12 @@
             return carry
 
         lax.fori_loop(0, lot // step, body, 0)
+
+    def quantize(i):
+        block = rows // BLOCKS
+        g, at = i * block // lot, i * block % lot
+        lines = pl.ds(pl.multiple_of(y * lot + at, block), block)
+        quantize_at(x_ref.at[here, g, lines, :])
 
     def run(z, op):
         kind = op[0]
@@ -312,6 +431,8 @@
         elif kind == "sent":
             way, o, c = op[1:]
             (cross(o, c) if way == "cross" else line(way, o, c)).wait_send()
+        elif kind == "quantize":
+            quantize(op[1])
         elif kind == "weights":
             weight(0, y, q_mine, op[1], peer).start()
         elif kind == "weights y":
@@ -322,7 +443,7 @@
             weight(1, other, q_across, op[1], across).wait_recv()
             weight(3, other, q_across, op[1], twin).start()
         elif kind == "add":
-            o, g = op[1:]
+            o, g, begin, end = op[1:]
             mine = x_ref.at[o, g, pl.ds(pl.multiple_of(y * lot, lot), lot), :]
 
             def body(n, carry):
@@ -332,9 +453,9 @@
                 partial(z, o, g, n, "up" if o > z else "down").start()
                 return carry
 
-            lax.fori_loop(0, PARTS, body, 0)
+            lax.fori_loop(begin, end, body, 0)
         elif kind == "finish":
-            g = op[1]
+            g, begin, end = op[2:]
             mine = x_ref.at[z, g, pl.ds(pl.multiple_of(y * lot, lot), lot), :]
             slots = ([z] if z > 0 else []) + ([LINE] if z < last else [])
 
@@ -349,7 +470,7 @@
                 )
                 return carry
 
-            lax.fori_loop(0, PARTS, body, 0)
+            lax.fori_loop(begin, end, body, 0)
         else:
             raise ValueError(kind)
 
@@ -396,26 +517,26 @@
     for target in targets:
         pl.semaphore_signal(barrier, inc=1, device_id=target, device_id_type=MESH)
 
-    def quantize(c):
-        g, i = c // PER, c % PER
-        if i == 0:
-            loads[g].wait()
-        quantize_at(chunk(here, c))
-
-    quantize(0)
+    for copy in loads[:GROUPS]:
+        copy.wait()
+    choices = ids_ref.shape[0]
+    names = lax.broadcasted_iota(jnp.int32, shares_ref.shape[1:], 0)
+    whole = sum(affinity_ref[i : i + 1, :] for i in range(choices))
+    shares_ref[here] = sum(
+        jnp.where(ids_ref[i : i + 1, :] == names, affinity_ref[i : i + 1, :] / whole, 0.0)
+        for i in range(choices)
+    )
+    for i in AHEAD:
+        quantize(i)
     pl.semaphore_wait(barrier, len(targets))
     play(FIRST)
     shares = []
     for step in range(1, LINE):
         target = {"ep": lax.rem(me + 2 * step, 2 * LINE)}
-        copy = remote(
-            share_ref, shares_ref.at[here], share_send.at[step], share_recv.at[step], target
-        )
+        mine = shares_ref.at[here]
+        copy = remote(mine, mine, share_send.at[step], share_recv.at[step], target)
         copy.start()
         shares.append(copy)
-    shares_ref[here] = share_ref[...]
-    for c in range(1, CHUNKS):
-        quantize(c)
     play(START)
     for copy in loads[GROUPS:]:
         copy.wait()
@@ -509,6 +630,7 @@
         return carry
 
     lax.fori_loop(0, STEPS, drain, 0)
+    play(LAST)
     for i in range(DOWN):
         weight(0, y, q_mine, i, peer).wait_send()
         weight(1, other, q_mine, i, across).wait_send()
@@ -516,7 +638,7 @@
         weight(3, other, q_across, i, twin).wait_send()
 
 
-def fused(tokens, share, w_gate, w_up, w_down):
+def fused(tokens, expert_ids, affinity, w_gate, w_up, w_down):
     rows, width = tokens.shape
     inner = w_gate.shape[2]
     lot = rows // GROUPS
@@ -527,7 +649,7 @@
     return pl.pallas_call(
         layer,
         out_shape=jax.ShapeDtypeStruct((rows, width), kind),
-        in_specs=[anywhere, inside, anywhere, anywhere, anywhere],
+        in_specs=[anywhere, inside, inside, anywhere, anywhere, anywhere],
         out_specs=inside,
         scratch_shapes=[
             pltpu.VMEM((LINE, GROUPS, 2 * lot, width), kind),
@@ -537,10 +659,10 @@
             pltpu.VMEM((LINE, GROUPS, 2 * lot, inner), kind),
             pltpu.VMEM((LINE, GROUPS, lot, inner), kind),
             pltpu.VMEM((LINE + 1, GROUPS, lot, width), kind),
-            pltpu.VMEM((LINE,) + share.shape, share.dtype),
+            pltpu.VMEM((LINE, 8, rows), affinity.dtype),
             dma((GROUPS + 3,)),
-            dma((2, LINE, CHUNKS)),
-            dma((LINE, CHUNKS)),
+            dma((2, LINE, PIECES)),
+            dma((LINE, PIECES)),
             dma((LINE, CHUNKS)),
             dma((LINE, CHUNKS)),
             dma((LINE, GROUPS)),
@@ -556,7 +678,7 @@
             collective_id=0, has_side_effects=True, vmem_limit_bytes=VMEM_LIMIT
         ),
         name="layer",
-    )(tokens, share, w_gate, w_up, w_down)
+    )(tokens, expert_ids.T, affinity.T, w_gate, w_up, w_down)
 
 
 def on_device(tokens, expert_ids, affinity, w_gate, w_up, w_down):
@@ -564,6 +686,14 @@
     experts = n // 2
     own = lax.axis_index("ep") // 2
     rows, width = tokens.shape
+    by_line = (
+        experts == LINE
+        and lax.axis_size("dp") == 4
+        and rows == LANES
+        and width % (PARTS * LANES) == 0
+    )
+    if by_line:
+        return fused(tokens, expert_ids, affinity, w_gate, w_up, w_down)
     weights = affinity / jnp.sum(affinity, axis=1, keepdims=True)
     padded = -(-experts // 8) * 8
     names = jnp.arange(padded, dtype=jnp.int32)[:, None]
@@ -571,14 +701,6 @@
         jnp.where(expert_ids[:, k][None, :] == names, weights[:, k][None, :], 0.0)
         for k in range(weights.shape[1])
     )
-    by_line = (
-        experts == LINE
-        and lax.axis_size("dp") == 4
-        and rows == LANES
-        and width % (PARTS * LANES) == 0
-    )
-    if by_line:
-        return fused(tokens, shares, w_gate, w_up, w_down)
     every = lax.all_gather(requantized(tokens), "ep", axis=0, tiled=False)
     shares = lax.all_gather(shares, "ep", axis=0, tiled=False)
     every = every.reshape(n * rows, width)

time: 286 us -> 235 us (0.82)
  Pallas kernels: 279 us -> 232 us
    pallas_call x1, Pallas kernels: 279 us -> 232 us  [fused(): pl.pallas_call(layer, out_shape=jax.ShapeDtypeStruct((rows, width), kind)...]
where the time goes in v2:
time: 235 us
  Pallas kernels  232 us (99%)
  local copies, waits for them, and re-layouts  2.85 us (1%)
    pallas_call x1, Pallas kernels, fused(): pl.pallas_call(layer, out_shape=jax.ShapeDtypeStruct((rows, width), kind)...  232 us

profile of v2, /device:TPU:16, one launch (start us, length us, event | category | flops | bytes accessed | tf_op | source)
XLA Modules:
  0.0 234.5 jit_solution(12737052827575140004)
XLA Ops:
  0.0 231.7 %layer.1 = bf16[128,7168]{1,0:T(8,128)(2,1)} custom-call(bf16[128,7168]{1,0:T(8,128)(2,1)} %tokens_ref.1, s32[2,128]{1,0:T(2,128)} %bitcast.2, f32[2,128]{1,0:T(2,128)} %bitcast.3, bf16[1,7168,512]{2,1,0:T(8,128)(2,1)} %gate_ref.1, bf16[1,7168,512]{2,1,0:T(8,128)(2,1)} %up_ref.1, bf16[1,512,7168]{2,1,0:T(8,128)(2,1)} %down_ref.1), custom_call_target="tpu_custom_call" | custom-call | tf_op jit(solution)/shard_map/layer/pallas_call | solution.py:649
  231.7 2.8 %copy.8 = bf16[128,7168]{1,0:T(8,128)(2,1)} copy(bf16[128,7168]{1,0:T(8,128)(2,1)} %layer.1) | data formatting | bytes 3670016

commit v3 on v2

--- a/solution.py
+++ b/solution.py
@@ -14,17 +14,21 @@
 VMEM_LIMIT = 62_000_000
 GROUPS = 2
 CHUNKS = 8
-EARLY = ()
+EARLY = (1, 5)
 PARTS = 7
 BLOCKS = 4
 LEAD = 0.5
 SLACK = 0.3
-DOWN = 2
+FAR = 2
+HOP = 2
+LATE = 1.4
+DOWN = 4
 PER = CHUNKS // GROUPS
 STEPS = LINE * GROUPS
 PIECES = CHUNKS + len(EARLY)
-AHEAD = sorted({c * BLOCKS // CHUNKS for c in (0, *EARLY)})
-ORDERS = ((3, 2, 1, 0), (3, 0, 2, 1), (0, 3, 1, 2), (0, 1, 2, 3))
+AHEAD = (0,)
+END = ((3, 0), (3, 1), (2, 0), (2, 1), (1, 0), (0, 0), (1, 1), (0, 1))
+INNER = ((3, 0), (3, 1), (0, 0), (0, 1), (2, 0), (2, 1), (1, 0), (1, 1))
 
 
 def requantized(tokens):
@@ -77,6 +81,10 @@
     return piece if piece < CHUNKS else EARLY[piece - CHUNKS]
 
 
+def early_at(z):
+    return EARLY if 0 < z < LINE - 1 else EARLY[:FAR]
+
+
 def in_order():
     return sorted(range(PIECES), key=lambda piece: (row_of(piece) // PER, piece))
 
@@ -84,24 +92,58 @@
 def down_line():
     ranks = {piece: rank for rank, piece in enumerate(in_order())}
     ready = {
-        z: {(z, piece): max(0, piece - CHUNKS + 2) for piece in range(PIECES)}
+        z: {(z, piece): max(0, 2 * (piece - CHUNKS) + 2) for piece in range(PIECES)}
         for z in range(LINE)
     }
     sends = {z: [] for z in range(LINE)}
     for slot in range(8 * PIECES):
         for z in range(LINE - 1, 0, -1):
-            able = [key for key, when in ready[z].items() if when <= slot]
+            able = [
+                key
+                for key, when in ready[z].items()
+                if when <= slot and (key[1] < CHUNKS or row_of(key[1]) in early_at(z - 1))
+            ]
             if able:
                 owner, piece = min(able, key=lambda key: (-key[0], ranks[key[1]]))
                 del ready[z][owner, piece]
                 sends[z].append((slot, owner, piece))
                 if z - 1 > 0:
-                    ready[z - 1][owner, piece] = slot + 1
+                    ready[z - 1][owner, piece] = slot + HOP
     return sends
 
 
+def turn(block):
+    early = sorted({c * BLOCKS // CHUNKS for c in EARLY} - set(AHEAD))
+    if block in early:
+        return 0.1 + early.index(block)
+    return block * CHUNKS / BLOCKS - 0.8
+
+
+def settled(c):
+    block = c * BLOCKS // CHUNKS
+    return 0 if block in AHEAD else turn(block) + 0.05
+
+
+def starts(z, moves, arrival):
+    latest, found = 0, []
+    for number, (slot, owner, piece) in enumerate(moves):
+        able = arrival.get((owner, piece), 0)
+        if owner == z:
+            tail = all(key[1] == z for key in moves[number:])
+            able = latest if tail and z in (1, LINE - 2) else max(0, slot - 1)
+            able = max(able, settled(row_of(piece)))
+            if piece >= CHUNKS:
+                able = max(able, 2 * (piece - CHUNKS) + 1.5)
+        latest = max(latest, able)
+        found.append((latest, owner, piece))
+    return found
+
+
 def flip(order):
-    return tuple(LINE - 1 - owner for owner in order)
+    return tuple((LINE - 1 - owner, g) for owner, g in order)
+
+
+ORDERS = (END, INNER, flip(INNER), flip(END))
 
 
 FIRST, START = -1, 0
@@ -123,22 +165,24 @@
 LAST = after(STEPS)
 
 
-def crossings(g):
-    return [c for c in range(g * PER, g * PER + PER) if c not in EARLY]
-
-
-def due(k):
-    each = [len(crossings(g)) + BACK for g in range(GROUPS)]
-    return LEAD + len(EARLY) + CHUNKS + k // GROUPS * sum(each) + sum(each[: k % GROUPS + 1])
-
-
-def ready_at(k):
-    return due(k) + 2
-
-
-def gap_of(time, least):
+def crossings(g, early):
+    return [c for c in range(g * PER, g * PER + PER) if c not in early]
+
+
+def due(k, z):
+    total = LEAD + CHUNKS + len(EARLY)
+    for o, g in ORDERS[z][: k + 1]:
+        total += len(crossings(g, EARLY if o == z else early_at(z))) + BACK
+    return total
+
+
+def ready_at(k, z):
+    return due(k, z) + 2
+
+
+def gap_of(time, least, z):
     k = least
-    while k < STEPS - 1 and due(k + 1) - SLACK < time:
+    while k < STEPS - 1 and due(k + 1, z) - SLACK < time:
         k += 1
     return k
 
@@ -152,14 +196,14 @@
         free = max(slot for slot, o, piece in down[LINE - 1 - z]) + 1
         todo = []
         for k in range(STEPS):
-            o, g = orders[z][k // GROUPS], k % GROUPS
+            o, g = orders[z][k]
             if o > z:
                 for n in range(PARTS):
-                    when = ready_at(k) + 0.1 * n
+                    when = ready_at(k, z) + 0.1 * n
                     place = k
                     if z > 0:
-                        place = gap_of(came[z][o, g, n], k)
-                        when = max(came[z][o, g, n], ready_at(place))
+                        place = gap_of(came[z][o, g, n], k, z)
+                        when = max(came[z][o, g, n], ready_at(place, z))
                     todo.append((place, when, o, g, n))
         for place, when, o, g, n in sorted(todo):
             free = max(free, when) + took
@@ -172,38 +216,45 @@
     last = LINE - 1
     down = down_line()
     up = {p: [(slot, last - o, c) for slot, o, c in down[last - p]] for p in range(LINE)}
-    moves = [(slot, "down", o, c) for slot, o, c in down[z]]
-    moves += [(slot, "up", o, c) for slot, o, c in up[z]]
-    arrival = {(z, c): 0 for c in range(CHUNKS)}
+    arrival = {(z, c): settled(c) for c in range(CHUNKS)}
     if z < last:
-        arrival.update({(o, c): slot + 1 for slot, o, c in down[z + 1]})
+        arrival.update({(o, c): slot + LATE for slot, o, c in down[z + 1]})
     if z > 0:
-        arrival.update({(o, c): slot + 1 for slot, o, c in up[z - 1]})
-    steps = [(ORDERS[z][k // GROUPS], k % GROUPS) for k in range(STEPS)]
-    chunks = [[(o, c) for c in crossings(g)] for o, g in steps]
+        arrival.update({(o, c): slot + LATE for slot, o, c in up[z - 1]})
+    moves = [(slot, "down", o, c) for slot, o, c in starts(z, down[z], arrival)]
+    moves += [(slot, "up", o, c) for slot, o, c in starts(z, up[z], arrival)]
+    steps = ORDERS[z]
+    chunks = [
+        [(o, c) for c in crossings(g, EARLY if o == z else early_at(z))] for o, g in steps
+    ]
     raw = []
 
     def add(place, rank, op):
         raw.append((place, rank, len(raw), op))
 
-    for i, c in enumerate(EARLY):
-        add(FIRST, 0.5, ("cross", z, c))
+    begun = {}
+    for c in EARLY:
+        block = c * BLOCKS // CHUNKS
+        begun[c] = 0.5 if block in AHEAD else turn(block) + 0.9
+        add(FIRST if block in AHEAD else START, begun[c], ("cross", z, c))
     for slot, way, o, piece in moves:
-        if slot == 0:
+        if slot == 0 and row_of(piece) * BLOCKS // CHUNKS in AHEAD:
             add(FIRST, 0, ("line", way, o, piece))
-        elif slot <= due(0) - SLACK:
+        elif slot <= due(0, z) - SLACK:
             add(START, slot, ("line", way, o, piece))
         else:
-            add(after(min(STEPS - 2, gap_of(slot, 0))), slot, ("line", way, o, piece))
+            k = min(STEPS - 2, gap_of(slot, 0, z))
+            place = middle(k) if slot <= due(k, z) + 0.6 else after(k)
+            add(place, 1 + slot / 100, ("line", way, o, piece))
     for i in range(BLOCKS):
         if i not in AHEAD:
-            add(START, i * CHUNKS / BLOCKS - 0.8, ("quantize", i))
+            add(START, turn(i), ("quantize", i))
     slow = CHUNKS / DOWN
     for i in range(DOWN):
-        add(FIRST, 1, ("weights", i))
+        add(FIRST if i == 0 else START, max(1, max(begun.values()) + 0.01), ("weights", i))
         add(START, len(EARLY) + (i + 1) * slow + 0.6, ("weights y", i))
         when = len(EARLY) + (i + 2) * slow + 1.1
-        add(START if when < due(0) else before(0), when, ("weights x", i))
+        add(START if when < due(0, z) else before(0), when, ("weights x", i))
     latest = 0
     for o, c in chunks[0] + chunks[1][:1]:
         latest = max(latest, arrival[o, c] + 0.2)
@@ -212,7 +263,7 @@
         o, g = steps[k]
         for c in range(g * PER, g * PER + PER):
             add(before(k), 0, ("arrived", o, c))
-            if c in EARLY and o != z:
+            if o != z and c in early_at(z):
                 add(before(k), 0.5, ("arrived", o, CHUNKS + EARLY.index(c)))
             else:
                 add(before(k), 1, ("crossed", o, c))
@@ -241,8 +292,8 @@
     for g in range(GROUPS):
         own = [k for k in range(STEPS) if steps[k] == (z, g)][0]
         for n in range(PARTS):
-            k = gap_of(came[z, g, n], own)
-            add(after(k), max(came[z, g, n], ready_at(k)), ("finish", z, g, n))
+            k = gap_of(came[z, g, n], own, z)
+            add(after(k), max(came[z, g, n], ready_at(k, z)), ("finish", z, g, n))
     waited, sent, freed = set(), [], set()
     done = collections.defaultdict(list)
     for place, rank, number, op in sorted(raw):
@@ -543,18 +594,18 @@
     for copy in shares:
         copy.wait()
 
-    def order(k):
-        b = k // GROUPS
+    def order(k, which):
         value = jnp.int32(0)
         for z in range(LINE):
-            for i in range(LINE):
-                value = jnp.where((here == z) & (b == i), ORDERS[z][i], value)
+            for i in range(STEPS):
+                if ORDERS[z][i][which]:
+                    value = jnp.where((here == z) & (k == i), ORDERS[z][i][which], value)
         return value
 
     half = inner // 2
 
     def step_of(k, carry):
-        o, g = order(k), lax.rem(k, GROUPS)
+        o, g = order(k, 0), order(k, 1)
         play_in(before, k)
 
         def hidden(j, c):

time: 235 us -> 207 us (0.88)
  Pallas kernels: 232 us -> 204 us
    pallas_call x1, Pallas kernels: 232 us -> 204 us  [fused(): pl.pallas_call(layer, out_shape=jax.ShapeDtypeStruct((rows, width), kind)...]
where the time goes in v3:
time: 207 us
  Pallas kernels  204 us (99%)
  local copies, waits for them, and re-layouts  2.85 us (1%)
    pallas_call x1, Pallas kernels, fused(): pl.pallas_call(layer, out_shape=jax.ShapeDtypeStruct((rows, width), kind)...  204 us

profile of v3, /device:TPU:16, one launch (start us, length us, event | category | flops | bytes accessed | tf_op | source)
XLA Modules:
  0.0 206.5 jit_solution(2952278761523711420)
XLA Ops:
  0.0 203.7 %layer.1 = bf16[128,7168]{1,0:T(8,128)(2,1)} custom-call(bf16[128,7168]{1,0:T(8,128)(2,1)} %tokens_ref.1, s32[2,128]{1,0:T(2,128)} %bitcast.2, f32[2,128]{1,0:T(2,128)} %bitcast.3, bf16[1,7168,512]{2,1,0:T(8,128)(2,1)} %gate_ref.1, bf16[1,7168,512]{2,1,0:T(8,128)(2,1)} %up_ref.1, bf16[1,512,7168]{2,1,0:T(8,128)(2,1)} %down_ref.1), custom_call_target="tpu_custom_call" | custom-call | tf_op jit(solution)/shard_map/layer/pallas_call | solution.py:700
  203.7 2.8 %copy.8 = bf16[128,7168]{1,0:T(8,128)(2,1)} copy(bf16[128,7168]{1,0:T(8,128)(2,1)} %layer.1) | data formatting | bytes 3670016

commit v4 on v3

--- a/solution.py
+++ b/solution.py
@@ -290,9 +290,8 @@
     for k, when, o, g, n in sorted(adds):
         add(after(k), when, ("add", o, g, n))
     for g in range(GROUPS):
-        own = [k for k in range(STEPS) if steps[k] == (z, g)][0]
         for n in range(PARTS):
-            k = gap_of(came[z, g, n], own, z)
+            k = STEPS - 1
             add(after(k), max(came[z, g, n], ready_at(k, z)), ("finish", z, g, n))
     waited, sent, freed = set(), [], set()
     done = collections.defaultdict(list)
@@ -345,6 +344,7 @@
     gate_ref,
     up_ref,
     down_ref,
+    result_ref,
     out_ref,
     x_ref,
     wg_ref,
@@ -420,7 +420,7 @@
     def weight(kind, half, q, i, target):
         place = wd_ref.at[half, rows_of(q, i), :]
         source = down_ref.at[0, rows_of(q, i), :] if kind == 0 else place
-        return remote(source, place, w_send.at[kind, i], w_recv.at[kind, i], target)
+        return remote(source, place, w_send.at[kind], w_recv.at[kind, i], target)
 
     q_mine, q_across = dp, lax.rem(dp + 2, 4)
     twin_dp = dp + 1 - 2 * lax.rem(dp, 2)
@@ -438,7 +438,7 @@
         return remote(
             source,
             got_ref.at[slot, g, :, columns],
-            part_send.at[o, g, n],
+            part_send.at[o, g],
             part_recv.at[slot, g, n],
             target,
         )
@@ -446,7 +446,7 @@
     def got_wait(slot, g, n):
         columns = pl.ds(pl.multiple_of(n * part, part), part)
         place = got_ref.at[slot, g, :, columns]
-        remote(place, place, part_send.at[0, g, n], part_recv.at[slot, g, n], peer).wait_recv()
+        remote(place, place, part_send.at[0, g], part_recv.at[slot, g, n], peer).wait_recv()
 
     def sum_into(target, at, sources):
         step = 16
@@ -519,6 +519,10 @@
                     at,
                     [mine] + [got_ref.at[slot, g] for slot in slots],
                 )
+                place = pl.ds(g * lot, lot)
+                pltpu.make_async_copy(
+                    out_ref.at[place, at], result_ref.at[place, at], local.at[GROUPS + 3]
+                ).start()
                 return carry
 
             lax.fori_loop(begin, end, body, 0)
@@ -559,17 +563,13 @@
 
     for g in range(GROUPS):
         load(tokens_ref.at[pl.ds(g * lot, lot), :], x_ref.at[here, g, own_rows, :])
-    load(gate_ref.at[0], wg_ref)
-    load(up_ref.at[0], wu_ref)
-    load(down_ref.at[0], wd_ref.at[y])
     barrier = pltpu.get_barrier_semaphore()
     targets = [{"ep": lax.rem(me + 2 * step, 2 * LINE)} for step in range(1, LINE)]
     targets += [peer, twin, across]
     for target in targets:
         pl.semaphore_signal(barrier, inc=1, device_id=target, device_id_type=MESH)
 
-    for copy in loads[:GROUPS]:
-        copy.wait()
+    loads[0].wait()
     choices = ids_ref.shape[0]
     names = lax.broadcasted_iota(jnp.int32, shares_ref.shape[1:], 0)
     whole = sum(affinity_ref[i : i + 1, :] for i in range(choices))
@@ -581,6 +581,11 @@
         quantize(i)
     pl.semaphore_wait(barrier, len(targets))
     play(FIRST)
+    load(gate_ref.at[0], wg_ref)
+    load(up_ref.at[0], wu_ref)
+    load(down_ref.at[0], wd_ref.at[y])
+    for copy in loads[1:GROUPS]:
+        copy.wait()
     shares = []
     for step in range(1, LINE):
         target = {"ep": lax.rem(me + 2 * step, 2 * LINE)}
@@ -672,21 +677,17 @@
 
         @pl.when(o != here)
         def _():
-            def body(n, c):
-                part_copy(o, o, g, n, peer).wait_send()
-                return c
-
-            lax.fori_loop(0, PARTS, body, 0)
+            whole = x_ref.at[o, g, own_rows, :]
+            remote(whole, whole, part_send.at[o, g], part_recv.at[o, g, 0], peer).wait_send()
 
         return carry
 
     lax.fori_loop(0, STEPS, drain, 0)
     play(LAST)
-    for i in range(DOWN):
-        weight(0, y, q_mine, i, peer).wait_send()
-        weight(1, other, q_mine, i, across).wait_send()
-        weight(2, other, q_mine, i, twin).wait_send()
-        weight(3, other, q_across, i, twin).wait_send()
+    pltpu.make_async_copy(out_ref, result_ref, local.at[GROUPS + 3]).wait()
+    for kind in range(4):
+        whole = wd_ref.at[0, pl.ds(0, quarter), :]
+        remote(whole, whole, w_send.at[kind], w_recv.at[kind, 0], peer).wait_send()
 
 
 def fused(tokens, expert_ids, affinity, w_gate, w_up, w_down):
@@ -701,8 +702,9 @@
         layer,
         out_shape=jax.ShapeDtypeStruct((rows, width), kind),
         in_specs=[anywhere, inside, inside, anywhere, anywhere, anywhere],
-        out_specs=inside,
+        out_specs=anywhere,
         scratch_shapes=[
+            pltpu.VMEM((rows, width), kind),
             pltpu.VMEM((LINE, GROUPS, 2 * lot, width), kind),
             pltpu.VMEM((width, inner), kind),
             pltpu.VMEM((width, inner), kind),
@@ -711,18 +713,18 @@
             pltpu.VMEM((LINE, GROUPS, lot, inner), kind),
             pltpu.VMEM((LINE + 1, GROUPS, lot, width), kind),
             pltpu.VMEM((LINE, 8, rows), affinity.dtype),
-            dma((GROUPS + 3,)),
+            dma((GROUPS + 4,)),
             dma((2, LINE, PIECES)),
             dma((LINE, PIECES)),
             dma((LINE, CHUNKS)),
             dma((LINE, CHUNKS)),
             dma((LINE, GROUPS)),
             dma((LINE, GROUPS)),
-            dma((LINE, GROUPS, PARTS)),
+            dma((LINE, GROUPS)),
             dma((LINE + 1, GROUPS, PARTS)),
             dma((LINE,)),
             dma((LINE,)),
-            dma((4, DOWN)),
+            dma((4,)),
             dma((4, DOWN)),
         ],
         compiler_params=pltpu.CompilerParams(

time: 207 us -> 205 us (level)
  no operation moved by 1% of the time
where the time goes in v4:
time: 205 us
  Pallas kernels  202 us (99%)
  local copies, waits for them, and re-layouts  2.85 us (1%)
    pallas_call x1, Pallas kernels, fused(): pl.pallas_call(layer, out_shape=jax.ShapeDtypeStruct((rows, width), kind)...  202 us

profile of v4, /device:TPU:16, one launch (start us, length us, event | category | flops | bytes accessed | tf_op | source)
XLA Modules:
  0.0 204.6 jit_solution(449885023022004010)
XLA Ops:
  0.0 201.7 %layer.1 = bf16[128,7168]{1,0:T(8,128)(2,1)} custom-call(bf16[128,7168]{1,0:T(8,128)(2,1)} %tokens_ref.1, s32[2,128]{1,0:T(2,128)} %bitcast.2, f32[2,128]{1,0:T(2,128)} %bitcast.3, bf16[1,7168,512]{2,1,0:T(8,128)(2,1)} %gate_ref.1, bf16[1,7168,512]{2,1,0:T(8,128)(2,1)} %up_ref.1, bf16[1,512,7168]{2,1,0:T(8,128)(2,1)} %down_ref.1), custom_call_target="tpu_custom_call" | custom-call | tf_op jit(solution)/shard_map/layer/pallas_call | solution.py:701
  201.7 2.8 %copy.8 = bf16[128,7168]{1,0:T(8,128)(2,1)} copy(bf16[128,7168]{1,0:T(8,128)(2,1)} %layer.1) | data formatting | bytes 3670016
